TPU v7x, 32 devices: a whole 2x2x4 slice. The times are simulated.
32 devices in a mesh: lat: 4 (over x, core), lon: 8 (over z, y).
Axes of the slice: x: 2, y: 2, z: 4, core: 2. Of those that a mesh axis runs over, the one named last changes fastest.
Arguments:
- tokens: bfloat16 [4, 48, 96, 512], P(None, 'lat', 'lon'), may hold values from -6 to 6
- region: int32 [4, 48, 96], P(None, 'lat', 'lon'), may hold values from 0 to 2
- norm_gain1: float32 [2, 512], replicated, may hold values from 0.25 to 1.75
- qkv_weight: bfloat16 [2, 512, 1536], replicated, may hold values from -3 to 3
- proj_weight: bfloat16 [2, 512, 512], replicated, may hold values from -0.25 to 0.25
- norm_gain2: float32 [2, 512], replicated, may hold values from 0.25 to 1.75
- up_weight: bfloat16 [2, 512, 2048], replicated, may hold values from -0.25 to 0.25
- down_weight: bfloat16 [2, 2048, 512], replicated, may hold values from -0.125 to 0.125
Outputs:
- result: bfloat16 [4, 48, 96, 512], P(None, 'lat', 'lon')
All inputs are finite; a program needn't handle non-finite values.
Results may differ from a plain program's by a relative error of at most 0.012.
Values may be sent and summed in bfloat16 or wider, within the bound.
A program may use at most 64 MiB of HBM per device.

v0:
```python
import functools

import jax
import jax.numpy as jnp
from jax import lax
from jax.experimental import pallas as pl
from jax.experimental.pallas import tpu as pltpu
from jax.sharding import PartitionSpec as P

HEADS = 8
WLEV = 2
WLAT = 6
WLON = 12
EPSILON = 1e-05
FAR = -1e30
MESH = pl.DeviceIdType.MESH
F32 = jnp.float32
BF16 = jnp.bfloat16


def normed(field, gain):
    mean = jnp.mean(field, axis=-1, keepdims=True)
    centered = field - mean
    variance = jnp.mean(centered * centered, axis=-1, keepdims=True)
    return (centered * lax.rsqrt(variance + EPSILON) * gain).astype(BF16)


def gelu(x):
    inner = x * (0.7978845608028654 + 0.035677408136300125 * (x * x))
    half = 0.5 * x
    return half + half * jnp.tanh(inner)


def dot(a, b):
    return jnp.dot(a, b, preferred_element_type=F32)


def dot_t(a, b):
    return lax.dot_general(a, b, (((1,), (1,)), ((), ())), preferred_element_type=F32)


def kernel(
    x_ref, e_ref, g1_ref, g2_ref, wqkv_hbm, wproj_hbm, wup_hbm, wdown_hbm, out_ref,
    own, shift, back, eshift, xs, qkv, heads, bias,
    wqkv, wproj, wup, wdown, wsem, fsend, frecv, bsend, brecv, esend, erecv,
):
    lat_count, lon_count = lax.axis_size("lat"), lax.axis_size("lon")
    lat, lon = lax.axis_index("lat"), lax.axis_index("lon")
    up = lax.rem(lat + lat_count - 1, lat_count)
    down = lax.rem(lat + 1, lat_count)
    left = lax.rem(lon + lon_count - 1, lon_count)
    right = lax.rem(lon + 1, lon_count)
    before = {"left": (lat, left), "up": (up, lon), "corner": (up, left)}
    after = {"left": (lat, right), "up": (down, lon), "corner": (down, right)}

    weights = [
        pltpu.make_async_copy(source.at[block], target.at[block], wsem.at[block * 4 + at])
        for block in range(2)
        for at, (source, target) in enumerate(
            ((wqkv_hbm, wqkv), (wproj_hbm, wproj), (wup_hbm, wup), (wdown_hbm, wdown))
        )
    ]
    weights[0].start()
    weights[1].start()

    barrier = pltpu.get_barrier_semaphore()
    for device in list(before.values()) + list(after.values()):
        pl.semaphore_signal(barrier, inc=1, device_id=device, device_id_type=MESH)

    moves = (
        (2, 0, 0, "left"),
        (0, 1, 1, "corner"),
        (4, 0, 1, "left"),
        (6, 1, 0, "left"),
        (1, 1, 2, "up"),
    )
    local = {(0, 2): 3, (0, 3): 5, (1, 3): 7}
    arrivals = {(move[1], move[2]): at for at, move in enumerate(moves)}

    def label_copy(at):
        atom, window, place, towards = moves[at]
        return pltpu.make_async_remote_copy(
            e_ref.at[atom], eshift.at[window, place], esend.at[at], erecv.at[at],
            device_id=before[towards], device_id_type=MESH,
        )

    def forward_copy(at):
        atom, window, place, towards = moves[at]
        return pltpu.make_async_remote_copy(
            own.at[atom], shift.at[window, place], fsend.at[at], frecv.at[at],
            device_id=before[towards], device_id_type=MESH,
        )

    def backward_copy(at):
        atom, window, place, towards = moves[at]
        return pltpu.make_async_remote_copy(
            back.at[window, place], out_ref.at[atom], bsend.at[at], brecv.at[at],
            device_id=after[towards], device_id_type=MESH,
        )

    span, features = xs.shape[1:]
    atom_size = span // 4
    part_size = span // 2
    pair = 128
    lane = lax.broadcasted_iota(jnp.int32, (1, pair), 1)
    low = lane < 64
    scale = 64 ** -0.5
    head_masks = (
        jnp.where(low, scale, 0.0).astype(BF16),
        jnp.where(low, 0.0, scale).astype(BF16),
    )

    def prepare(block, at, pieces, marks):
        index = 2 * block + at
        marks = jnp.concatenate([piece.astype(F32) for piece in marks], axis=0)
        half = low if block == 0 else jnp.logical_not(low)
        query = (marks * jnp.where(half, FAR, 0.0)).astype(BF16)
        bias[index] = dot_t(query, (1.0 - marks).astype(BF16))
        x = jnp.concatenate([piece.astype(F32) for piece in pieces], axis=0)
        xs[index] = x
        n1 = normed(x, g1_ref[block : block + 1, :])
        if at == 0:
            weights[block * 4].wait()
        qkv[index] = dot(n1, wqkv[block]).astype(BF16)

    def part(block, at, which, first):
        index = 2 * block + at
        rows = slice(which * part_size, (which + 1) * part_size)
        ones = jnp.ones((span, pair), BF16)
        offset = bias[index, rows, :]
        offset = jnp.concatenate([offset, offset], axis=0)
        for column in range(0, features, pair):
            query = qkv[index, rows, column : column + pair]
            key = qkv[index, :, features + column : features + column + pair]
            value = qkv[index, :, 2 * features + column : 2 * features + column + pair]
            value = jnp.concatenate([value, ones], axis=1)
            query = jnp.concatenate([query * head_masks[0], query * head_masks[1]], axis=0)
            scores = dot_t(query, key) + offset
            peak = jnp.max(scores, axis=-1, keepdims=True)
            weight = jnp.exp(scores - peak).astype(BF16)
            total = dot(weight, value)
            total = total[:, :pair] / total[:, pair:]
            heads[index, rows, column : column + pair] = jnp.where(
                low, total[:part_size], total[part_size:]
            ).astype(BF16)
        if first:
            weights[block * 4 + 1].wait()
        h = xs[index, rows, :] + dot(heads[index, rows, :], wproj[block])
        n2 = normed(h, g2_ref[block : block + 1, :])
        if first:
            weights[block * 4 + 2].wait()
            weights[block * 4 + 3].wait()
        hidden = wup.shape[2]
        step = 512
        for column in range(0, hidden, step):
            inner = gelu(dot(n2, wup[block, :, column : column + step])).astype(BF16)
            h = h + dot(inner, wdown[block, column : column + step, :])
        return h[:atom_size].astype(BF16), h[atom_size:].astype(BF16)

    def prepare_first(u):
        atoms = (4 * u, 4 * u + 2, 4 * u + 1, 4 * u + 3)
        prepare(0, u, [x_ref[a] for a in atoms], [e_ref[a] for a in atoms])

    def part_first(u, which, first=False):
        own[4 * u + which], own[4 * u + 2 + which] = part(0, u, which, first)

    prepare_first(0)
    weights[2].start()
    weights[3].start()
    part_first(0, 0, True)
    pl.semaphore_wait(barrier, 6)
    for at in range(5):
        label_copy(at).start()
    forward_copy(0).start()
    forward_copy(1).start()
    for at in range(4, 8):
        weights[at].start()
    prepare_first(1)
    part_first(1, 0)
    forward_copy(2).start()
    forward_copy(3).start()
    part_first(0, 1)
    forward_copy(4).start()
    part_first(1, 1)

    def prepare_second(w):
        pieces, marks = [], []
        for place in range(4):
            if (w, place) in arrivals:
                label_copy(arrivals[w, place]).wait_recv()
                forward_copy(arrivals[w, place]).wait_recv()
        for place in range(4):
            if (w, place) in arrivals:
                pieces.append(shift[w, place])
                marks.append(eshift[w, place])
            else:
                pieces.append(own[local[w, place]])
                marks.append(e_ref[local[w, place]])
        prepare(1, w, pieces, marks)

    def part_second(w, which, first=False):
        results = part(1, w, which, first)
        for at in range(2):
            place = 2 * which + at
            if (w, place) in local:
                out_ref[local[w, place]] = results[at]
            else:
                back[w, place] = results[at]
        for at in range(2):
            if (w, 2 * which + at) in arrivals:
                backward_copy(arrivals[w, 2 * which + at]).start()

    prepare_second(0)
    part_second(0, 0, True)
    prepare_second(1)
    part_second(1, 0)
    part_second(1, 1)
    part_second(0, 1)
    for at in range(5):
        backward_copy(at).wait_recv()
    for at in range(5):
        label_copy(at).wait_send()
        forward_copy(at).wait_send()
        backward_copy(at).wait_send()


def to_atoms(field):
    levels, row_count, column_count = field.shape[:3]
    trailing = tuple(field.shape[3:])
    half_row, half_column = WLAT // 2, WLON // 2
    shaped = field.reshape(
        (levels, row_count // half_row, half_row, column_count // half_column, half_column)
        + trailing
    )
    order = (1, 3, 0, 2, 4) + tuple(range(5, 5 + len(trailing)))
    return jnp.transpose(shaped, order).reshape(
        (-1, levels * half_row * half_column) + trailing
    )


def from_atoms(atoms, levels, row_count, column_count):
    trailing = tuple(atoms.shape[2:])
    half_row, half_column = WLAT // 2, WLON // 2
    shaped = atoms.reshape(
        (row_count // half_row, column_count // half_column, levels, half_row, half_column)
        + trailing
    )
    order = (2, 0, 3, 1, 4) + tuple(range(5, 5 + len(trailing)))
    return jnp.transpose(shaped, order).reshape((levels, row_count, column_count) + trailing)


def per_device(
    tokens, region, norm_gain1, qkv_weight, proj_weight, norm_gain2, up_weight, down_weight
):
    levels, row_count, column_count, features = tokens.shape
    hidden = up_weight.shape[2]
    x = to_atoms(tokens)
    atoms, size, _ = x.shape
    span = 4 * size

    level = jnp.arange(levels, dtype=jnp.int32)[:, None, None]
    row = (lax.axis_index("lat") * row_count + jnp.arange(row_count, dtype=jnp.int32))[None, :, None]
    pair_first = level // WLEV
    rolled_level = (level + levels - WLEV // 2) % levels
    wrapped_level = (rolled_level >= levels - WLEV // 2).astype(jnp.int32)
    wrapped_row = (row < WLAT // 2).astype(jnp.int32)
    first_class = region * 2 + pair_first
    second_class = ((region * 2 + rolled_level // WLEV) * 2 + wrapped_level) * 2 + wrapped_row
    classes = jnp.stack([first_class, second_class + 64], axis=-1)
    classes = to_atoms(classes)
    lane = jnp.arange(128, dtype=jnp.int32)
    marks = (
        (classes[:, :, :1] == lane) | (classes[:, :, 1:] == lane)
    ).astype(BF16)

    vmem = pl.BlockSpec(memory_space=pltpu.VMEM)
    hbm = pl.BlockSpec(memory_space=pl.ANY)
    out = pl.pallas_call(
        kernel,
        out_shape=jax.ShapeDtypeStruct((atoms, size, features), BF16),
        in_specs=[vmem] * 4 + [hbm] * 4,
        out_specs=vmem,
        scratch_shapes=[
            pltpu.VMEM((atoms, size, features), BF16),
            pltpu.VMEM((2, 4, size, features), BF16),
            pltpu.VMEM((2, 4, size, features), BF16),
            pltpu.VMEM((2, 4, size, 128), BF16),
            pltpu.VMEM((4, span, features), F32),
            pltpu.VMEM((4, span, 3 * features), BF16),
            pltpu.VMEM((4, span, features), BF16),
            pltpu.VMEM((4, span, span), F32),
            pltpu.VMEM(qkv_weight.shape, BF16),
            pltpu.VMEM(proj_weight.shape, BF16),
            pltpu.VMEM(up_weight.shape, BF16),
            pltpu.VMEM(down_weight.shape, BF16),
            pltpu.SemaphoreType.DMA((8,)),
            pltpu.SemaphoreType.DMA((5,)),
            pltpu.SemaphoreType.DMA((5,)),
            pltpu.SemaphoreType.DMA((5,)),
            pltpu.SemaphoreType.DMA((5,)),
            pltpu.SemaphoreType.DMA((5,)),
            pltpu.SemaphoreType.DMA((5,)),
        ],
        compiler_params=pltpu.CompilerParams(
            collective_id=0, has_side_effects=True, vmem_limit_bytes=50 * 1024 * 1024
        ),
    )(x, marks, norm_gain1, norm_gain2, qkv_weight, proj_weight, up_weight, down_weight)
    return from_atoms(out, levels, row_count, column_count)


def solution(mesh):
    return jax.shard_map(
        per_device,
        mesh=mesh,
        in_specs=(P(None, "lat", "lon", None), P(None, "lat", "lon"), P(), P(), P(), P(), P(), P()),
        out_specs=P(None, "lat", "lon", None),
        check_vma=False,
    )
```

profile of v0, /device:TPU:0, one launch (start us, length us, event | category | flops | bytes accessed | tf_op | source)
XLA Modules:
  0.0 38.1 jit_solution(13606005750275088441)
XLA Ops:
  0.0 0.0 copy-start.2
  0.0 0.0 copy-start
  0.0 0.0 copy-start.1
  0.0 0.9 %multiply_add_fusion = (s32[4,12,12]{2,0,1:T(4,128)S(1)}, s32[4,12,12]{2,0,1:T(4,128)S(1)}) fusion(s32[4,12,12]{2,0,1:T(4,128)} %param.9, s32[4]{0:T(128)S(1)} %get-tuple-element.10, s32[12]{0:T(128)S(1)} %compare_convert_fusion, s32[4]{0:T(128)S(1)} %compare_convert_fusion.1, s32[4]{0:T(128)S(1)} %get-tuple-element.9), kind=kLoop, calls=%fused_computation.7 | loop fusion | flops 4608 | bytes 7008 | tf_op jit(solution)/shard_map/add | solution.py:267
  1.0 0.1 stack.9
  1.1 0.1 stack.10
  1.3 0.1 reshape.128
  1.4 0.2 fusion.1.e_ref
  1.6 1.6 %copy.24 = bf16[4,4,3,2,6,512]{5,3,1,4,2,0:T(2,128)(2,1)S(1)} copy(bf16[4,4,3,2,6,512]{5,0,4,3,2,1:T(4,128)(2,1)} %bitcast.24) | data formatting | bytes 1179648 | tf_op jit(solution)/shard_map/reshape | solution.py:231
  3.2 0.2 reshape.127
  3.4 0.2 copy.20.x_ref
  3.6 0.0 copy-done.2
  3.6 0.0 copy-done
  3.6 0.0 copy-done.1
  3.7 32.7 %shard_map.82 = bf16[8,72,512]{2,1,0:T(8,128)(2,1)S(1)} custom-call(bf16[8,72,512]{2,1,0:T(8,128)(2,1)S(1)} %copy.20.x_ref, bf16[8,72,128]{2,1,0:T(8,128)(2,1)S(1)} %fusion.1.e_ref, f32[2,512]{1,0:T(2,128)S(1)} %copy-done.1, f32[2,512]{1,0:T(2,128)S(1)} %copy-done.2, bf16[2,512,1536]{2,1,0:T(8,128)(2,1)} %wqkv_hbm.1, bf16[2,512,512]{2,1,0:T(8,128)(2,1)S(1)} %copy-done, ...), custom_call_target="tpu_custom_call" | custom-call | tf_op jit(solution)/shard_map/pallas_call | solution.py:278
  36.4 0.2 copy.21
  36.6 0.2 reshape.129
  36.8 1.3 %copy.22 = bf16[4,4,3,2,6,512]{5,0,4,3,2,1:T(4,128)(2,1)} copy(bf16[4,4,3,2,6,512]{5,3,1,4,2,0:T(2,128)(2,1)S(1)} %bitcast.22) | data formatting | bytes 1179648 | tf_op jit(solution)/shard_map/transpose | solution.py:249
  (7 shorter events, 0.1 us)
Async XLA Ops:
  0.0 3.6 %copy-start.2 = (f32[2,512]{1,0:T(2,128)S(1)}, f32[2,512]{1,0:T(2,128)}, u32[]{:S(2)}) copy-start(f32[2,512]{1,0:T(2,128)} %g2_ref.1) | copy-start | bytes 12292
  0.0 3.6 %copy-start = (bf16[2,512,512]{2,1,0:T(8,128)(2,1)S(1)}, bf16[2,512,512]{2,1,0:T(8,128)(2,1)}, u32[]{:S(2)}) copy-start(bf16[2,512,512]{2,1,0:T(8,128)(2,1)} %wproj_hbm.1) | copy-start | bytes 3145732
  0.0 3.6 %copy-start.1 = (f32[2,512]{1,0:T(2,128)S(1)}, f32[2,512]{1,0:T(2,128)}, u32[]{:S(2)}) copy-start(f32[2,512]{1,0:T(2,128)} %g1_ref.1) | copy-start | bytes 12292
where the time goes:
time: 38.3 us; the launch traced here: 38.1 us
  Pallas kernels  32.7 us (85%)
  local copies, waits for them, and re-layouts  4.03 us (11%)
  other arithmetic  1.19 us (3%)
    pallas_call x1, Pallas kernels, per_device(): pl.pallas_call(kernel, out_shape=jax.ShapeDtypeStruct((atoms, size, featu...  32.7 us
    reshape x1, local copies, waits for them, and re-layouts, to_atoms(): field.reshape((levels, row_count // half_row, half_row, column_count // h...  1.57 us
    transpose x1, local copies, waits for them, and re-layouts, from_atoms(): jnp.transpose(shaped, order)  1.27 us
    add x1, other arithmetic, per_device(): first_class = region * 2 + pair_first  0.91 us

commit v1 on v0

--- a/solution.py
+++ b/solution.py
@@ -41,7 +41,7 @@
 
 def kernel(
     x_ref, e_ref, g1_ref, g2_ref, wqkv_hbm, wproj_hbm, wup_hbm, wdown_hbm, out_ref,
-    own, shift, back, eshift, xs, qkv, heads, bias,
+    own, shift, back, eshift, xs, qkv, heads, marks_q, marks_k, inner,
     wqkv, wproj, wup, wdown, wsem, fsend, frecv, bsend, brecv, esend, erecv,
 ):
     lat_count, lon_count = lax.axis_size("lat"), lax.axis_size("lon")
@@ -99,9 +99,13 @@
         )
 
     span, features = xs.shape[1:]
-    atom_size = span // 4
-    part_size = span // 2
+    half_span = span // 2
+    size = span // 4
+    piece = span // 8
+    level_size = span // 16
     pair = 128
+    hidden = wup.shape[2]
+    step = 256
     lane = lax.broadcasted_iota(jnp.int32, (1, pair), 1)
     low = lane < 64
     scale = 64 ** -0.5
@@ -110,64 +114,96 @@
         jnp.where(low, 0.0, scale).astype(BF16),
     )
 
-    def prepare(block, at, pieces, marks):
+    def to_pairs(block, pieces):
+        pieces = [value.astype(F32) for value in pieces]
+        if block == 0:
+            order = [value[:piece] for value in pieces] + [value[piece:] for value in pieces]
+        else:
+            order = [value[level_size : level_size + piece] for value in pieces]
+            for value in pieces:
+                order += [value[level_size + piece :], value[:level_size]]
+        return jnp.concatenate(order, axis=0)
+
+    def from_pairs(block, first, second):
+        if block == 0:
+            order = [first, second]
+        else:
+            order = [second[level_size:], first, second[:level_size]]
+        return jnp.concatenate(order, axis=0).astype(BF16)
+
+    def prepare(block, at, pieces, marks_in):
         index = 2 * block + at
-        marks = jnp.concatenate([piece.astype(F32) for piece in marks], axis=0)
+        marks = to_pairs(block, marks_in)
         half = low if block == 0 else jnp.logical_not(low)
-        query = (marks * jnp.where(half, FAR, 0.0)).astype(BF16)
-        bias[index] = dot_t(query, (1.0 - marks).astype(BF16))
-        x = jnp.concatenate([piece.astype(F32) for piece in pieces], axis=0)
+        marks_q[index] = (marks * jnp.where(half, FAR, 0.0)).astype(BF16)
+        marks_k[index] = (1.0 - marks).astype(BF16)
+        x = to_pairs(block, pieces)
         xs[index] = x
         n1 = normed(x, g1_ref[block : block + 1, :])
         if at == 0:
             weights[block * 4].wait()
         qkv[index] = dot(n1, wqkv[block]).astype(BF16)
 
-    def part(block, at, which, first):
+    def attend(block, at):
         index = 2 * block + at
-        rows = slice(which * part_size, (which + 1) * part_size)
-        ones = jnp.ones((span, pair), BF16)
-        offset = bias[index, rows, :]
-        offset = jnp.concatenate([offset, offset], axis=0)
-        for column in range(0, features, pair):
-            query = qkv[index, rows, column : column + pair]
-            key = qkv[index, :, features + column : features + column + pair]
-            value = qkv[index, :, 2 * features + column : 2 * features + column + pair]
-            value = jnp.concatenate([value, ones], axis=1)
-            query = jnp.concatenate([query * head_masks[0], query * head_masks[1]], axis=0)
-            scores = dot_t(query, key) + offset
-            peak = jnp.max(scores, axis=-1, keepdims=True)
-            weight = jnp.exp(scores - peak).astype(BF16)
-            total = dot(weight, value)
-            total = total[:, :pair] / total[:, pair:]
-            heads[index, rows, column : column + pair] = jnp.where(
-                low, total[:part_size], total[part_size:]
-            ).astype(BF16)
+        ones = jnp.ones((half_span, pair), BF16)
+        for rows in (slice(0, half_span), slice(half_span, span)):
+            mark_q = marks_q[index, rows, :]
+            mark_q = jnp.concatenate([mark_q, mark_q], axis=0)
+            mark_k = marks_k[index, rows, :]
+            for column in range(0, features, pair):
+                query = qkv[index, rows, column : column + pair]
+                key = qkv[index, rows, features + column : features + column + pair]
+                value = qkv[index, rows, 2 * features + column : 2 * features + column + pair]
+                value = jnp.concatenate([value, ones], axis=1)
+                query = jnp.concatenate([query * head_masks[0], query * head_masks[1]], axis=0)
+                scores = dot_t(
+                    jnp.concatenate([query, mark_q], axis=1),
+                    jnp.concatenate([key, mark_k], axis=1),
+                )
+                peak = jnp.max(scores, axis=-1, keepdims=True)
+                weight = jnp.exp(scores - peak).astype(BF16)
+                total = dot(weight, value)
+                over = jnp.where(low, total[:half_span, :pair], total[half_span:, :pair])
+                under = jnp.where(low, total[:half_span, pair:], total[half_span:, pair:])
+                heads[index, rows, column : column + pair] = over / under
+
+    def mlp(block, parts, first=False):
+        slots = []
+        for at, which in parts:
+            for start in (which * size, half_span + which * size):
+                slots.append((2 * block + at, slice(start, start + size)))
+        gathered = jnp.concatenate([heads[index, rows, :] for index, rows in slots], axis=0)
         if first:
             weights[block * 4 + 1].wait()
-        h = xs[index, rows, :] + dot(heads[index, rows, :], wproj[block])
+        h = jnp.concatenate([xs[index, rows, :] for index, rows in slots], axis=0)
+        h = h + dot(gathered.astype(BF16), wproj[block])
         n2 = normed(h, g2_ref[block : block + 1, :])
         if first:
             weights[block * 4 + 2].wait()
             weights[block * 4 + 3].wait()
-        hidden = wup.shape[2]
-        step = 512
+        count = h.shape[0]
         for column in range(0, hidden, step):
-            inner = gelu(dot(n2, wup[block, :, column : column + step])).astype(BF16)
-            h = h + dot(inner, wdown[block, column : column + step, :])
-        return h[:atom_size].astype(BF16), h[atom_size:].astype(BF16)
+            inner[:count, column : column + step] = gelu(
+                dot(n2, wup[block, :, column : column + step]).astype(BF16)
+            )
+        h = h + dot(inner[:count, :], wdown[block])
+        results = []
+        for start in range(0, count, 2 * size):
+            one, two = h[start : start + size], h[start + size : start + 2 * size]
+            results.append(from_pairs(block, one[:piece], two[:piece]))
+            results.append(from_pairs(block, one[piece:], two[piece:]))
+        return results
 
     def prepare_first(u):
         atoms = (4 * u, 4 * u + 2, 4 * u + 1, 4 * u + 3)
         prepare(0, u, [x_ref[a] for a in atoms], [e_ref[a] for a in atoms])
 
-    def part_first(u, which, first=False):
-        own[4 * u + which], own[4 * u + 2 + which] = part(0, u, which, first)
-
     prepare_first(0)
     weights[2].start()
     weights[3].start()
-    part_first(0, 0, True)
+    attend(0, 0)
+    own[0], own[2] = mlp(0, [(0, 0)], True)
     pl.semaphore_wait(barrier, 6)
     for at in range(5):
         label_copy(at).start()
@@ -176,12 +212,12 @@
     for at in range(4, 8):
         weights[at].start()
     prepare_first(1)
-    part_first(1, 0)
+    attend(0, 1)
+    own[4], own[6] = mlp(0, [(1, 0)])
     forward_copy(2).start()
     forward_copy(3).start()
-    part_first(0, 1)
+    own[1], own[3], own[5], own[7] = mlp(0, [(0, 1), (1, 1)])
     forward_copy(4).start()
-    part_first(1, 1)
 
     def prepare_second(w):
         pieces, marks = [], []
@@ -198,24 +234,25 @@
                 marks.append(e_ref[local[w, place]])
         prepare(1, w, pieces, marks)
 
-    def part_second(w, which, first=False):
-        results = part(1, w, which, first)
-        for at in range(2):
-            place = 2 * which + at
+    def mlp_second(parts, first=False):
+        results = mlp(1, parts, first)
+        places = [(w, 2 * which + at) for w, which in parts for at in range(2)]
+        for (w, place), result in zip(places, results):
             if (w, place) in local:
-                out_ref[local[w, place]] = results[at]
+                out_ref[local[w, place]] = result
             else:
-                back[w, place] = results[at]
-        for at in range(2):
-            if (w, 2 * which + at) in arrivals:
-                backward_copy(arrivals[w, 2 * which + at]).start()
+                back[w, place] = result
+        for w, place in places:
+            if (w, place) in arrivals:
+                backward_copy(arrivals[w, place]).start()
 
     prepare_second(0)
-    part_second(0, 0, True)
+    attend(1, 0)
+    mlp_second([(0, 0)], True)
     prepare_second(1)
-    part_second(1, 0)
-    part_second(1, 1)
-    part_second(0, 1)
+    attend(1, 1)
+    mlp_second([(1, 0)])
+    mlp_second([(1, 1), (0, 1)])
     for at in range(5):
         backward_copy(at).wait_recv()
     for at in range(5):
@@ -287,8 +324,10 @@
             pltpu.VMEM((2, 4, size, 128), BF16),
             pltpu.VMEM((4, span, features), F32),
             pltpu.VMEM((4, span, 3 * features), BF16),
-            pltpu.VMEM((4, span, features), BF16),
-            pltpu.VMEM((4, span, span), F32),
+            pltpu.VMEM((4, span, features), F32),
+            pltpu.VMEM((4, span, 128), BF16),
+            pltpu.VMEM((4, span, 128), BF16),
+            pltpu.VMEM((span, hidden), BF16),
             pltpu.VMEM(qkv_weight.shape, BF16),
             pltpu.VMEM(proj_weight.shape, BF16),
             pltpu.VMEM(up_weight.shape, BF16),

time: 38.3 us -> 34.7 us (0.906)
  Pallas kernels: 32.7 us -> 29.2 us
    pallas_call x1, Pallas kernels: 32.7 us -> 29.2 us  [per_device(): pl.pallas_call(kernel, out_shape=jax.ShapeDtypeStruct((atoms, size, featu...]
where the time goes in v1:
time: 34.7 us; the launch traced here: 34.5 us
  Pallas kernels  29.2 us (84%)
  local copies, waits for them, and re-layouts  4.03 us (12%)
  other arithmetic  1.19 us (3%)
    pallas_call x1, Pallas kernels, per_device(): pl.pallas_call(kernel, out_shape=jax.ShapeDtypeStruct((atoms, size, featu...  29.2 us
    reshape x1, local copies, waits for them, and re-layouts, to_atoms(): field.reshape((levels, row_count // half_row, half_row, column_count // h...  1.57 us
    transpose x1, local copies, waits for them, and re-layouts, from_atoms(): jnp.transpose(shaped, order)  1.27 us
    add x1, other arithmetic, per_device(): first_class = region * 2 + pair_first  0.91 us

profile of v1, /device:TPU:0, one launch (start us, length us, event | category | flops | bytes accessed | tf_op | source)
XLA Modules:
  0.0 34.5 jit_solution(6681681447914871751)
XLA Ops:
  0.0 0.0 copy-start.2
  0.0 0.0 copy-start
  0.0 0.0 copy-start.1
  0.0 0.9 %multiply_add_fusion = (s32[4,12,12]{2,0,1:T(4,128)S(1)}, s32[4,12,12]{2,0,1:T(4,128)S(1)}) fusion(s32[4,12,12]{2,0,1:T(4,128)} %param.9, s32[4]{0:T(128)S(1)} %get-tuple-element.10, s32[12]{0:T(128)S(1)} %compare_convert_fusion, s32[4]{0:T(128)S(1)} %compare_convert_fusion.1, s32[4]{0:T(128)S(1)} %get-tuple-element.9), kind=kLoop, calls=%fused_computation.7 | loop fusion | flops 4608 | bytes 7008 | tf_op jit(solution)/shard_map/add | solution.py:304
  1.0 0.1 stack.9
  1.1 0.1 stack.10
  1.3 0.1 reshape.128
  1.4 0.2 fusion.1.e_ref
  1.6 1.6 %copy.24 = bf16[4,4,3,2,6,512]{5,3,1,4,2,0:T(2,128)(2,1)S(1)} copy(bf16[4,4,3,2,6,512]{5,0,4,3,2,1:T(4,128)(2,1)} %bitcast.24) | data formatting | bytes 1179648 | tf_op jit(solution)/shard_map/reshape | solution.py:268
  3.2 0.2 reshape.127
  3.4 0.2 copy.20.x_ref
  3.6 0.0 copy-done.2
  3.6 0.0 copy-done
  3.6 0.0 copy-done.1
  3.7 29.2 %shard_map.82 = bf16[8,72,512]{2,1,0:T(8,128)(2,1)S(1)} custom-call(bf16[8,72,512]{2,1,0:T(8,128)(2,1)S(1)} %copy.20.x_ref, bf16[8,72,128]{2,1,0:T(8,128)(2,1)S(1)} %fusion.1.e_ref, f32[2,512]{1,0:T(2,128)S(1)} %copy-done.1, f32[2,512]{1,0:T(2,128)S(1)} %copy-done.2, bf16[2,512,1536]{2,1,0:T(8,128)(2,1)} %wqkv_hbm.1, bf16[2,512,512]{2,1,0:T(8,128)(2,1)S(1)} %copy-done, ...), custom_call_target="tpu_custom_call" | custom-call | tf_op jit(solution)/shard_map/pallas_call | solution.py:315
  32.8 0.2 copy.21
  33.0 0.2 reshape.129
  33.2 1.3 %copy.22 = bf16[4,4,3,2,6,512]{5,0,4,3,2,1:T(4,128)(2,1)} copy(bf16[4,4,3,2,6,512]{5,3,1,4,2,0:T(2,128)(2,1)S(1)} %bitcast.22) | data formatting | bytes 1179648 | tf_op jit(solution)/shard_map/transpose | solution.py:286
  (7 shorter events, 0.1 us)
Async XLA Ops:
  0.0 3.6 %copy-start.2 = (f32[2,512]{1,0:T(2,128)S(1)}, f32[2,512]{1,0:T(2,128)}, u32[]{:S(2)}) copy-start(f32[2,512]{1,0:T(2,128)} %g2_ref.1) | copy-start | bytes 12292
  0.0 3.6 %copy-start = (bf16[2,512,512]{2,1,0:T(8,128)(2,1)S(1)}, bf16[2,512,512]{2,1,0:T(8,128)(2,1)}, u32[]{:S(2)}) copy-start(bf16[2,512,512]{2,1,0:T(8,128)(2,1)} %wproj_hbm.1) | copy-start | bytes 3145732
  0.0 3.6 %copy-start.1 = (f32[2,512]{1,0:T(2,128)S(1)}, f32[2,512]{1,0:T(2,128)}, u32[]{:S(2)}) copy-start(f32[2,512]{1,0:T(2,128)} %g1_ref.1) | copy-start | bytes 12292

commit v2 on v0

v2 whole, which is shorter than its diff:
```python
import jax
import jax.numpy as jnp
import numpy as np
from jax import lax
from jax.experimental import pallas as pl
from jax.experimental.pallas import tpu as pltpu
from jax.sharding import PartitionSpec as P

HEADS = 8
WLEV = 2
WLAT = 6
WLON = 12
EPSILON = 1e-05
FAR = -1e30
LANES = 128
MESH = pl.DeviceIdType.MESH
F32 = jnp.float32
BF16 = jnp.bfloat16


def normed(field, gain):
    mean = jnp.mean(field, axis=-1, keepdims=True)
    centered = field - mean
    variance = jnp.mean(centered * centered, axis=-1, keepdims=True)
    return (centered * lax.rsqrt(variance + EPSILON) * gain).astype(BF16)


def gelu(x):
    inner = x * (0.7978845608028654 + 0.035677408136300125 * (x * x))
    half = 0.5 * x
    return half + half * jnp.tanh(inner)


def dot(a, b):
    return jnp.dot(a, b, preferred_element_type=F32)


def dot_t(a, b):
    return lax.dot_general(a, b, (((1,), (1,)), ((), ())), preferred_element_type=F32)


HALF_ROW, HALF_COLUMN = WLAT // 2, WLON // 2
CELL = HALF_ROW * HALF_COLUMN
QUARTER = WLEV * CELL
SPOT = 16


def label_tables(levels):
    windows = levels // WLEV
    select = np.zeros((2, windows * 4 * QUARTER, LANES), np.float32)
    column = np.zeros((windows * 4 * QUARTER, LANES), np.float32)
    rows = 4 * HALF_ROW * levels
    for block in range(2):
        for token in range(select.shape[1]):
            group, rest = divmod(token, 4 * QUARTER)
            place, rest = divmod(rest, QUARTER)
            spot, level = divmod(rest, WLEV)
            row, col = divmod(spot, HALF_COLUMN)
            level = (group * WLEV + level + block * (WLEV // 2)) % levels
            select[block, token, (place * HALF_ROW + row) * levels + level] = 1
            column[token, col + HALF_COLUMN * (place // 2)] = 1
            column[token, SPOT] = 1
            if block == 1:
                select[block, token, rows] = level < WLEV // 2
                select[block, token, rows + 1] = place in (1, 2)
    return jnp.asarray(select, BF16), jnp.asarray(column, F32)


def kernel(
    x_hbm, e_hbm, select_hbm, column_hbm, g1_hbm, g2_hbm,
    wqkv_hbm, wproj_hbm, wup_hbm, wdown_hbm, out_ref,
    xin, region, select, column, g1, g2, regions, own, shift, side, corner, below,
    xs, qkv, heads, marks_q, marks_k, inner, flat, cross, wide, ready, o_send, o_back,
    wqkv, wproj, wup, wdown, wsem, isem, fsend, frecv, esend, erecv, osend, orecv, bsend, brecv,
):
    lat_count, lon_count = lax.axis_size("lat"), lax.axis_size("lon")
    lat, lon = lax.axis_index("lat"), lax.axis_index("lon")
    up = lax.rem(lat + lat_count - 1, lat_count)
    down = lax.rem(lat + 1, lat_count)
    left = lax.rem(lon + lon_count - 1, lon_count)
    right = lax.rem(lon + 1, lon_count)
    before = {"left": (lat, left), "up": (up, lon), "corner": (up, left)}
    after = {"left": (lat, right), "up": (down, lon), "corner": (down, right)}

    spots, lane_tiles, levels, lanes = xin.shape
    features = lane_tiles * lanes
    span = xs.shape[1]
    group = span // 2
    half = group // 2
    hidden = wup.shape[2]
    step = 256
    columns = 2 * HALF_COLUMN
    window_spots = spots // 2

    weights = [
        pltpu.make_async_copy(source.at[block], target.at[block], wsem.at[block * 4 + at])
        for block in range(2)
        for at, (source, target) in enumerate(
            ((wqkv_hbm, wqkv), (wproj_hbm, wproj), (wup_hbm, wup), (wdown_hbm, wdown))
        )
    ]
    halves = [pl.ds(u * window_spots, window_spots) for u in range(2)]
    inputs = [
        pltpu.make_async_copy(source, target, isem.at[at])
        for at, (source, target) in enumerate(
            (
                (x_hbm.at[halves[0]], xin.at[halves[0]]),
                (x_hbm.at[halves[1]], xin.at[halves[1]]),
                (e_hbm, region),
                (select_hbm, select),
                (column_hbm, column),
                (g1_hbm, g1),
                (g2_hbm, g2),
            )
        )
    ]
    inputs[0].start()
    for at in (5, 2, 3, 4):
        inputs[at].start()
    weights[0].start()
    inputs[1].start()
    inputs[6].start()
    for at in range(1, 4):
        weights[at].start()

    barrier = pltpu.get_barrier_semaphore()
    for device in list(before.values()) + list(after.values()):
        pl.semaphore_signal(barrier, inc=1, device_id=device, device_id_type=MESH)

    moves = (
        (2, 0, 0, "left"),
        (0, 1, 1, "corner"),
        (4, 0, 1, "left"),
        (6, 1, 0, "left"),
        (1, 1, 2, "up"),
    )
    local = {(0, 2): 3, (0, 3): 5, (1, 3): 7}
    arrivals = {(move[1], move[2]): at for at, move in enumerate(moves)}
    returns = ((6, 0, "left"), (0, 1, "corner"), (1, 2, "up"))

    def remote(source, target, send, recv, device):
        return pltpu.make_async_remote_copy(
            source, target, send, recv, device_id=device, device_id_type=MESH
        )

    labels = [
        remote(region.at[HALF_ROW:], side, esend.at[0], erecv.at[0], before["left"]),
        remote(region.at[:HALF_ROW], corner, esend.at[1], erecv.at[1], before["corner"]),
        remote(region.at[:HALF_ROW], below, esend.at[2], erecv.at[2], before["up"]),
    ]
    forward = [
        remote(own.at[atom], shift.at[window, place], fsend.at[at], frecv.at[at], before[towards])
        for at, (atom, window, place, towards) in enumerate(moves)
    ]
    outward = remote(o_send, o_back, osend.at[0], orecv.at[0], after["left"])

    def first_spot(atom, row):
        return ((atom // 2) * HALF_ROW + row) * columns + (atom % 2) * HALF_COLUMN

    backward = [
        remote(
            ready.at[at, pl.ds(row * HALF_COLUMN, HALF_COLUMN)],
            out_ref.at[pl.ds(first_spot(atom, row), HALF_COLUMN)],
            bsend.at[at * HALF_ROW + row],
            brecv.at[at * HALF_ROW + row],
            after[towards],
        )
        for at, (atom, place, towards) in enumerate(returns)
        for row in range(HALF_ROW)
    ]

    lane = lax.broadcasted_iota(jnp.int32, (1, lanes), 1)
    lane_value = lane.astype(F32)
    low = lane < 64
    scale = 64 ** -0.5
    head_masks = (
        jnp.where(low, scale, 0.0).astype(BF16),
        jnp.where(low, 0.0, scale).astype(BF16),
    )

    def tile(at):
        return slice(at * lanes, (at + 1) * lanes)

    def mark(block, at, places):
        index = 2 * block + at
        count = HALF_ROW * levels
        regions[index] = jnp.zeros(regions.shape[1:], F32)
        for place, (source, row) in enumerate(places):
            for r in range(HALF_ROW):
                start = place * count + r * levels
                regions[index, start : start + levels, :columns] = source[row + r].astype(F32)
        if block == 1:
            wrapped = jnp.where(lat == lat_count - 1, 8.0, 0.0) if at == 1 else 0.0
            regions[index, 4 * count : 4 * count + 1, :] = jnp.where(lane == SPOT, 4.0, 0.0)
            regions[index, 4 * count + 1 : 4 * count + 2, :] = jnp.where(lane == SPOT, wrapped, 0.0)
        value = dot(select[block], regions[index].astype(BF16)) * column[...]
        same = jnp.sum(value, axis=-1, keepdims=True) == lane_value
        marks_q[index] = jnp.where(same, FAR, 0.0).astype(BF16)
        marks_k[index] = jnp.where(same, 0.0, 1.0).astype(BF16)

    def project(block, at):
        index = 2 * block + at
        n1 = normed(xs[index], g1[block : block + 1, :])
        if at == 0:
            weights[block * 4].wait()
        qkv[index] = dot(n1, wqkv[block]).astype(BF16)

    cut = -(-half // 16) * 16

    def attend(block, at, which):
        index = 2 * block + at
        first, last = ((0, cut), (cut, group), (0, group))[which]
        size = last - first
        ones = jnp.ones((group, lanes), BF16)
        for start in (0, group):
            rows = slice(start + first, start + last)
            keys = slice(start, start + group)
            mark_q = marks_q[index, rows, :]
            mark_q = jnp.concatenate([mark_q, mark_q], axis=0)
            mark_k = marks_k[index, keys, :]
            for at_tile in range(lane_tiles):
                query = qkv[index, rows, tile(at_tile)]
                key = qkv[index, keys, tile(lane_tiles + at_tile)]
                value = qkv[index, keys, tile(2 * lane_tiles + at_tile)]
                value = jnp.concatenate([value, ones], axis=1)
                query = jnp.concatenate([query * head_masks[0], query * head_masks[1]], axis=0)
                scores = dot_t(
                    jnp.concatenate([query, mark_q], axis=1),
                    jnp.concatenate([key, mark_k], axis=1),
                )
                peak = jnp.max(scores, axis=-1, keepdims=True)
                weight = jnp.exp(scores - peak).astype(BF16)
                total = dot(weight, value)
                over = jnp.where(low, total[:size, :lanes], total[size:, :lanes])
                under = jnp.where(low, total[:size, lanes:], total[size:, lanes:])
                heads[index, rows, tile(at_tile)] = over / under

    def gather(source, parts):
        pieces = []
        for index, which in parts:
            for start in (which * half, group + which * half):
                pieces.append(source[index, start : start + half, :])
        return jnp.concatenate(pieces, axis=0)

    def mlp(block, h, mixed, first=False):
        if first:
            weights[block * 4 + 1].wait()
        h = h + dot(mixed, wproj[block])
        n2 = normed(h, g2[block : block + 1, :])
        if first:
            weights[block * 4 + 2].wait()
        count = h.shape[0]
        for at in range(0, hidden, step):
            inner[:count, at : at + step] = gelu(
                dot(n2, wup[block, :, at : at + step]).astype(BF16)
            )
        if first:
            weights[block * 4 + 3].wait()
        return h + dot(inner[:count, :], wdown[block])

    def relevel(slot, h, shifts, targets, stride):
        for at in range(lane_tiles):
            flat[slot, at] = h[:, tile(at)]
        for place, target in enumerate(targets):
            for at in range(lane_tiles):
                for group_at in range(2):
                    for lev in range(WLEV):
                        source = group_at * half + place * QUARTER + lev
                        target[at, pl.ds(shifts[group_at][lev], CELL, stride=stride)] = flat[
                            slot, at, pl.ds(source, CELL, stride=WLEV)
                        ]

    def finish_first(slot, h, atoms):
        targets = [cross.at[slot, place] for place in range(2)]
        relevel(slot, h, ((QUARTER + 1, 0), (1, QUARTER)), targets, WLEV)
        for place, atom in enumerate(atoms):
            for at in range(lane_tiles):
                own[atom, :, tile(at)] = cross[slot, place, at].astype(BF16)

    def finish_second(slot, h, results):
        targets = [wide.at[slot, place] for place in range(2)]
        relevel(slot, h, ((1, 2), (3, 0)), targets, levels)
        for place, result in enumerate(results):
            for spot in range(CELL):
                row, col = divmod(spot, HALF_COLUMN)
                for at in range(lane_tiles):
                    value = wide[slot, place, at, spot * levels : (spot + 1) * levels].astype(BF16)
                    if result[0] == "out":
                        out_ref[first_spot(result[1], row) + col, at] = value
                    else:
                        ready[result[1], spot, at] = value
            if result[0] == "send":
                for row in range(HALF_ROW):
                    backward[result[1] * HALF_ROW + row].start()

    def load_first(u):
        inputs[u].wait()
        for spot in range(window_spots):
            row, col = divmod(spot, columns)
            place = (col // HALF_COLUMN) * 2 + row // HALF_ROW
            at_spot = (row % HALF_ROW) * HALF_COLUMN + col % HALF_COLUMN
            start = place * QUARTER + at_spot * WLEV
            for at in range(lane_tiles):
                value = xin[u * window_spots + spot, at].astype(F32)
                for group_at in range(2):
                    xs[u, group_at * group + start : group_at * group + start + WLEV, tile(at)] = (
                        value[group_at * WLEV : (group_at + 1) * WLEV]
                    )

    def own_regions(u):
        places = [(region, u * WLAT), (region, u * WLAT + HALF_ROW)]
        return places + places

    def load_second(w, places):
        for place in places:
            if (w, place) in arrivals:
                forward[arrivals[w, place]].wait_recv()
                value = shift[w, place].astype(F32)
            else:
                value = own[local[w, place]].astype(F32)
            for group_at in range(2):
                start = group_at * group + place * QUARTER
                xs[2 + w, start : start + QUARTER, :] = value[
                    group_at * QUARTER : (group_at + 1) * QUARTER
                ]

    load_first(0)
    inputs[2].wait()
    inputs[3].wait()
    inputs[4].wait()
    mark(0, 0, own_regions(0))
    inputs[5].wait()
    project(0, 0)
    pl.semaphore_wait(barrier, 6)
    for copy in labels:
        copy.start()
    for at in range(4, 8):
        weights[at].start()
    attend(0, 0, 0)
    inputs[6].wait()
    h = mlp(0, gather(xs, [(0, 0)]), gather(heads, [(0, 0)]).astype(BF16), True)
    finish_first(0, h, (0, 2))
    forward[0].start()
    forward[1].start()
    load_first(1)
    mark(0, 1, own_regions(1))
    project(0, 1)
    attend(0, 1, 0)
    h = mlp(0, gather(xs, [(1, 0)]), gather(heads, [(1, 0)]).astype(BF16))
    finish_first(1, h, (4, 6))
    forward[2].start()
    forward[3].start()
    attend(0, 0, 1)
    attend(0, 1, 1)
    parts = [(0, 1), (1, 1)]
    h = mlp(0, gather(xs, parts), gather(heads, parts).astype(BF16))
    finish_first(0, h[:group], (1, 3))
    forward[4].start()
    finish_first(1, h[group:], (5, 7))

    for copy in labels:
        copy.wait_recv()
    load_second(0, (2, 3))
    mark(1, 0, [(side, 0), (side, HALF_ROW), (region, HALF_ROW), (region, 2 * HALF_ROW)])
    mark(1, 1, [(side, 2 * HALF_ROW), (corner, 0), (below, 0), (region, 3 * HALF_ROW)])
    load_second(0, (0, 1))
    project(1, 0)
    attend(1, 0, 0)
    o_send[...] = gather(heads, [(2, 0)]).astype(BF16)
    outward.start()
    attend(1, 0, 1)
    load_second(1, (0, 1, 2, 3))
    project(1, 1)
    attend(1, 1, 0)
    h = mlp(1, gather(xs, [(3, 0)]), gather(heads, [(3, 0)]).astype(BF16), True)
    finish_second(0, h, (("send", 0), ("send", 1)))
    attend(1, 1, 1)
    parts = [(3, 1), (2, 1)]
    h = mlp(1, gather(xs, parts), gather(heads, parts).astype(BF16))
    finish_second(1, h[:group], (("send", 2), ("out", 7)))
    finish_second(0, h[group:], (("out", 3), ("out", 5)))
    pieces = [own[2].astype(F32), own[4].astype(F32)]
    residual = jnp.concatenate(
        [piece[:QUARTER] for piece in pieces] + [piece[QUARTER:] for piece in pieces], axis=0
    )
    outward.wait_recv()
    h = mlp(1, residual, o_back[...])
    finish_second(1, h, (("out", 2), ("out", 4)))
    for copy in backward:
        copy.wait_recv()
    for copy in labels + forward + [outward] + backward:
        copy.wait_send()


def per_device(
    tokens, region, norm_gain1, qkv_weight, proj_weight, norm_gain2, up_weight, down_weight
):
    levels, row_count, column_count, features = tokens.shape
    hidden = up_weight.shape[2]
    lane_tiles = features // LANES
    spots = row_count * column_count
    quarter_rows = levels * CELL
    span = 4 * quarter_rows
    group = span // 2
    x = jnp.transpose(tokens.reshape(levels, spots, lane_tiles, LANES), (1, 2, 0, 3))
    marks = jnp.transpose(region, (1, 0, 2))
    select, column = label_tables(levels)

    vmem = pl.BlockSpec(memory_space=pltpu.VMEM)
    hbm = pl.BlockSpec(memory_space=pl.ANY)
    dma = pltpu.SemaphoreType.DMA
    out = pl.pallas_call(
        kernel,
        out_shape=jax.ShapeDtypeStruct(x.shape, BF16),
        in_specs=[hbm] * 10,
        out_specs=vmem,
        scratch_shapes=[
            pltpu.VMEM(x.shape, BF16),
            pltpu.VMEM(marks.shape, jnp.int32),
            pltpu.VMEM(select.shape, BF16),
            pltpu.VMEM(column.shape, F32),
            pltpu.VMEM(norm_gain1.shape, F32),
            pltpu.VMEM(norm_gain2.shape, F32),
            pltpu.VMEM((4, LANES, LANES), F32),
            pltpu.VMEM((8, quarter_rows, features), BF16),
            pltpu.VMEM((2, 4, quarter_rows, features), BF16),
            pltpu.VMEM((row_count - HALF_ROW,) + marks.shape[1:], jnp.int32),
            pltpu.VMEM((HALF_ROW,) + marks.shape[1:], jnp.int32),
            pltpu.VMEM((HALF_ROW,) + marks.shape[1:], jnp.int32),
            pltpu.VMEM((4, span, features), F32),
            pltpu.VMEM((4, span, 3 * features), BF16),
            pltpu.VMEM((4, span, features), F32),
            pltpu.VMEM((4, span, LANES), BF16),
            pltpu.VMEM((4, span, LANES), BF16),
            pltpu.VMEM((span, hidden), BF16),
            pltpu.VMEM((2, lane_tiles, group, LANES), F32),
            pltpu.VMEM((2, 2, lane_tiles, quarter_rows, LANES), F32),
            pltpu.VMEM((2, 2, lane_tiles, quarter_rows, LANES), F32),
            pltpu.VMEM((3, CELL) + x.shape[1:], BF16),
            pltpu.VMEM((group, features), BF16),
            pltpu.VMEM((group, features), BF16),
            pltpu.VMEM(qkv_weight.shape, BF16),
            pltpu.VMEM(proj_weight.shape, BF16),
            pltpu.VMEM(up_weight.shape, BF16),
            pltpu.VMEM(down_weight.shape, BF16),
            dma((8,)),
            dma((7,)),
            dma((5,)),
            dma((5,)),
            dma((3,)),
            dma((3,)),
            dma((1,)),
            dma((1,)),
            dma((3 * HALF_ROW,)),
            dma((3 * HALF_ROW,)),
        ],
        compiler_params=pltpu.CompilerParams(
            collective_id=0, has_side_effects=True, vmem_limit_bytes=56 * 1024 * 1024
        ),
    )(
        x, marks, select, column, norm_gain1, norm_gain2,
        qkv_weight, proj_weight, up_weight, down_weight,
    )
    return jnp.transpose(out, (2, 0, 1, 3)).reshape(tokens.shape)


def solution(mesh):
    return jax.shard_map(
        per_device,
        mesh=mesh,
        in_specs=(P(None, "lat", "lon", None), P(None, "lat", "lon"), P(), P(), P(), P(), P(), P()),
        out_specs=P(None, "lat", "lon", None),
        check_vma=False,
    )
```

time: 38.3 us -> 33 us (0.86)
  Pallas kernels: 32.7 us -> 30.7 us
  local copies, waits for them, and re-layouts: 4.03 us -> 2.13 us
  other arithmetic: 1.19 us -> 0 us
    reshape x5 -> x0, local copies, waits for them, and re-layouts: 2.33 us -> none  [the longest x1 1.57 us: to_atoms(): field.reshape((levels, row_count // half_row, half_row, column_count // h...]
    unnamed x6 -> x1, local copies, waits for them, and re-layouts: 0.01 us -> 2.13 us
    pallas_call x1, Pallas kernels: 32.7 us -> 30.7 us  [per_device(): pl.pallas_call(kernel, out_shape=jax.ShapeDtypeStruct(x.shape, BF16), in_...]
    transpose x1 -> x0, local copies, waits for them, and re-layouts: 1.27 us -> none  [from_atoms(): jnp.transpose(shaped, order)]
    add x1 -> x0, other arithmetic: 0.91 us -> none  [per_device(): first_class = region * 2 + pair_first]
where the time goes in v2:
time: 33 us; the launch traced here: 32.8 us
  Pallas kernels  30.7 us (93%)
  local copies, waits for them, and re-layouts  2.13 us (6%)
    pallas_call x1, Pallas kernels, per_device(): pl.pallas_call(kernel, out_shape=jax.ShapeDtypeStruct(x.shape, BF16), in_...  30.7 us
    unnamed x1, local copies, waits for them, and re-layouts  2.13 us

profile of v2, /device:TPU:0, one launch (start us, length us, event | category | flops | bytes accessed | tf_op | source)
XLA Modules:
  0.0 32.8 jit_solution(5226415146143642284)
XLA Ops:
  0.0 30.7 %shard_map.100 = bf16[144,4,4,128]{3,2,1,0:T(4,128)(2,1)} custom-call(bf16[144,4,4,128]{3,2,1,0:T(4,128)(2,1)} %bitcast.8, s32[12,4,12]{2,1,0:T(4,128)} %bitcast.9, bf16[2,288,128]{2,1,0:T(8,128)(2,1)} %constant.4.clone.select_hbm, f32[288,128]{1,0:T(8,128)} %constant.5.clone.column_hbm, f32[2,512]{1,0:T(2,128)} %g1_hbm.1, f32[2,512]{1,0:T(2,128)} %g2_hbm.1, ...), custom_call_target="tpu_custom_call" | custom-call | tf_op jit(solution)/shard_map/pallas_call | solution.py:412
  30.7 2.1 %copy.12 = bf16[4,12,12,512]{3,0,2,1:T(4,128)(2,1)} copy(bf16[4,12,12,512]{3,0,2,1:T(4,128)(2,1)} %bitcast.7) | data formatting | bytes 1179648

commit v3 on v2

--- a/solution.py
+++ b/solution.py
@@ -205,23 +205,18 @@
             weights[block * 4].wait()
         qkv[index] = dot(n1, wqkv[block]).astype(BF16)
 
-    cut = -(-half // 16) * 16
-
-    def attend(block, at, which):
+    def attend(block, at):
         index = 2 * block + at
-        first, last = ((0, cut), (cut, group), (0, group))[which]
-        size = last - first
         ones = jnp.ones((group, lanes), BF16)
         for start in (0, group):
-            rows = slice(start + first, start + last)
-            keys = slice(start, start + group)
+            rows = slice(start, start + group)
             mark_q = marks_q[index, rows, :]
             mark_q = jnp.concatenate([mark_q, mark_q], axis=0)
-            mark_k = marks_k[index, keys, :]
+            mark_k = marks_k[index, rows, :]
             for at_tile in range(lane_tiles):
                 query = qkv[index, rows, tile(at_tile)]
-                key = qkv[index, keys, tile(lane_tiles + at_tile)]
-                value = qkv[index, keys, tile(2 * lane_tiles + at_tile)]
+                key = qkv[index, rows, tile(lane_tiles + at_tile)]
+                value = qkv[index, rows, tile(2 * lane_tiles + at_tile)]
                 value = jnp.concatenate([value, ones], axis=1)
                 query = jnp.concatenate([query * head_masks[0], query * head_masks[1]], axis=0)
                 scores = dot_t(
@@ -231,8 +226,8 @@
                 peak = jnp.max(scores, axis=-1, keepdims=True)
                 weight = jnp.exp(scores - peak).astype(BF16)
                 total = dot(weight, value)
-                over = jnp.where(low, total[:size, :lanes], total[size:, :lanes])
-                under = jnp.where(low, total[:size, lanes:], total[size:, lanes:])
+                over = jnp.where(low, total[:group, :lanes], total[group:, :lanes])
+                under = jnp.where(low, total[:group, lanes:], total[group:, lanes:])
                 heads[index, rows, tile(at_tile)] = over / under
 
     def gather(source, parts):
@@ -336,7 +331,7 @@
         copy.start()
     for at in range(4, 8):
         weights[at].start()
-    attend(0, 0, 0)
+    attend(0, 0)
     inputs[6].wait()
     h = mlp(0, gather(xs, [(0, 0)]), gather(heads, [(0, 0)]).astype(BF16), True)
     finish_first(0, h, (0, 2))
@@ -345,13 +340,11 @@
     load_first(1)
     mark(0, 1, own_regions(1))
     project(0, 1)
-    attend(0, 1, 0)
+    attend(0, 1)
     h = mlp(0, gather(xs, [(1, 0)]), gather(heads, [(1, 0)]).astype(BF16))
     finish_first(1, h, (4, 6))
     forward[2].start()
     forward[3].start()
-    attend(0, 0, 1)
-    attend(0, 1, 1)
     parts = [(0, 1), (1, 1)]
     h = mlp(0, gather(xs, parts), gather(heads, parts).astype(BF16))
     finish_first(0, h[:group], (1, 3))
@@ -365,16 +358,14 @@
     mark(1, 1, [(side, 2 * HALF_ROW), (corner, 0), (below, 0), (region, 3 * HALF_ROW)])
     load_second(0, (0, 1))
     project(1, 0)
-    attend(1, 0, 0)
+    attend(1, 0)
     o_send[...] = gather(heads, [(2, 0)]).astype(BF16)
     outward.start()
-    attend(1, 0, 1)
     load_second(1, (0, 1, 2, 3))
     project(1, 1)
-    attend(1, 1, 0)
+    attend(1, 1)
     h = mlp(1, gather(xs, [(3, 0)]), gather(heads, [(3, 0)]).astype(BF16), True)
     finish_second(0, h, (("send", 0), ("send", 1)))
-    attend(1, 1, 1)
     parts = [(3, 1), (2, 1)]
     h = mlp(1, gather(xs, parts), gather(heads, parts).astype(BF16))
     finish_second(1, h[:group], (("send", 2), ("out", 7)))
@@ -392,6 +383,21 @@
         copy.wait_send()
 
 
+def settle(source, target, sems):
+    chunks = sems.shape[0]
+    size = source.shape[0] // chunks
+    copies = [
+        pltpu.make_async_copy(
+            source.at[pl.ds(at * size, size)], target.at[pl.ds(at * size, size)], sems.at[at]
+        )
+        for at in range(chunks)
+    ]
+    for copy in copies:
+        copy.start()
+    for copy in copies:
+        copy.wait()
+
+
 def per_device(
     tokens, region, norm_gain1, qkv_weight, proj_weight, norm_gain2, up_weight, down_weight
 ):
@@ -411,7 +417,7 @@
     dma = pltpu.SemaphoreType.DMA
     out = pl.pallas_call(
         kernel,
-        out_shape=jax.ShapeDtypeStruct(x.shape, BF16),
+        out_shape=pltpu.VMEM(x.shape, BF16),
         in_specs=[hbm] * 10,
         out_specs=vmem,
         scratch_shapes=[
@@ -455,12 +461,20 @@
             dma((3 * HALF_ROW,)),
         ],
         compiler_params=pltpu.CompilerParams(
-            collective_id=0, has_side_effects=True, vmem_limit_bytes=56 * 1024 * 1024
+            collective_id=0, has_side_effects=True, vmem_limit_bytes=54 * 1024 * 1024
         ),
     )(
         x, marks, select, column, norm_gain1, norm_gain2,
         qkv_weight, proj_weight, up_weight, down_weight,
     )
+    out = pl.pallas_call(
+        settle,
+        out_shape=jax.ShapeDtypeStruct(x.shape, BF16),
+        in_specs=[vmem],
+        out_specs=hbm,
+        scratch_shapes=[dma((8,))],
+        compiler_params=pltpu.CompilerParams(vmem_limit_bytes=2 * 1024 * 1024),
+    )(out)
     return jnp.transpose(out, (2, 0, 1, 3)).reshape(tokens.shape)
 
 

time: 33 us -> 29.4 us (0.89)
  local copies, waits for them, and re-layouts: 2.13 us -> 0 us
  Pallas kernels: 30.7 us -> 29.2 us
    unnamed x1 -> x0, local copies, waits for them, and re-layouts: 2.13 us -> none
    pallas_call x1 -> x2, Pallas kernels: 30.7 us -> 29.2 us  [the longest x1 28.3 us: per_device(): pl.pallas_call(kernel, out_shape=pltpu.VMEM(x.shape, BF16), in_specs=[hbm...]
where the time goes in v3:
time: 29.4 us; the launch traced here: 29.2 us
  Pallas kernels  29.2 us (99%)
    pallas_call x1, Pallas kernels, per_device(): pl.pallas_call(kernel, out_shape=pltpu.VMEM(x.shape, BF16), in_specs=[hbm...  28.3 us
    pallas_call x1, Pallas kernels, per_device(): pl.pallas_call(settle, out_shape=jax.ShapeDtypeStruct(x.shape, BF16), in_...  0.88 us

profile of v3, /device:TPU:0, one launch (start us, length us, event | category | flops | bytes accessed | tf_op | source)
XLA Modules:
  0.0 29.2 jit_solution(1347293027301583625)
XLA Ops:
  0.0 28.3 %shard_map.100.source = bf16[144,4,4,128]{3,2,1,0:T(4,128)(2,1)S(1)} custom-call(bf16[144,4,4,128]{3,2,1,0:T(4,128)(2,1)} %bitcast.7, s32[12,4,12]{2,1,0:T(4,128)} %bitcast.8, bf16[2,288,128]{2,1,0:T(8,128)(2,1)} %constant.4.clone.select_hbm, f32[288,128]{1,0:T(8,128)} %constant.5.clone.column_hbm, f32[2,512]{1,0:T(2,128)} %g1_hbm.1, f32[2,512]{1,0:T(2,128)} %g2_hbm.1, ...), custom_call_target="tpu_custom_call" | custom-call | tf_op jit(solution)/shard_map/pallas_call | solution.py:418
  28.3 0.9 %shard_map.101 = bf16[144,4,4,128]{3,2,1,0:T(4,128)(2,1)} custom-call(bf16[144,4,4,128]{3,2,1,0:T(4,128)(2,1)S(1)} %shard_map.100.source), custom_call_target="tpu_custom_call" | custom-call | tf_op jit(solution)/shard_map/pallas_call | solution.py:470

commit v4 on v3

--- a/solution.py
+++ b/solution.py
@@ -118,10 +118,6 @@
     for at in (5, 2, 3, 4):
         inputs[at].start()
     weights[0].start()
-    inputs[1].start()
-    inputs[6].start()
-    for at in range(1, 4):
-        weights[at].start()
 
     barrier = pltpu.get_barrier_semaphore()
     for device in list(before.values()) + list(after.values()):
@@ -198,37 +194,70 @@
         marks_q[index] = jnp.where(same, FAR, 0.0).astype(BF16)
         marks_k[index] = jnp.where(same, 0.0, 1.0).astype(BF16)
 
-    def project(block, at):
+    def project(block, at, spans, first=False):
         index = 2 * block + at
-        n1 = normed(xs[index], g1[block : block + 1, :])
-        if at == 0:
+        rows = jnp.concatenate([xs[index, span_at, :] for span_at in spans], axis=0)
+        n1 = normed(rows, g1[block : block + 1, :])
+        if first:
             weights[block * 4].wait()
-        qkv[index] = dot(n1, wqkv[block]).astype(BF16)
-
-    def attend(block, at):
+        if first and block == 0:
+            inputs[1].start()
+            inputs[6].start()
+            for later in (1, 2, 3):
+                weights[later].start()
+        mixed = dot(n1, wqkv[block]).astype(BF16)
+        start = 0
+        for span_at in spans:
+            size = span_at.stop - span_at.start
+            qkv[index, span_at, :] = mixed[start : start + size]
+            start += size
+
+    whole = (slice(0, span),)
+    near = (slice(half, group), slice(group + half, span))
+    far = (slice(0, half), slice(group, group + half))
+
+    cut = -(-half // 16) * 16
+
+    def attend(block, at, first=0, last=0):
         index = 2 * block + at
+        last = last or group
+        size = last - first
         ones = jnp.ones((group, lanes), BF16)
-        for start in (0, group):
+        jobs = [(start, at_tile) for start in (0, group) for at_tile in range(lane_tiles)]
+        scored, weighted = {}, {}
+
+        def score(start, at_tile):
             rows = slice(start, start + group)
-            mark_q = marks_q[index, rows, :]
-            mark_q = jnp.concatenate([mark_q, mark_q], axis=0)
-            mark_k = marks_k[index, rows, :]
-            for at_tile in range(lane_tiles):
-                query = qkv[index, rows, tile(at_tile)]
-                key = qkv[index, rows, tile(lane_tiles + at_tile)]
-                value = qkv[index, rows, tile(2 * lane_tiles + at_tile)]
-                value = jnp.concatenate([value, ones], axis=1)
-                query = jnp.concatenate([query * head_masks[0], query * head_masks[1]], axis=0)
-                scores = dot_t(
-                    jnp.concatenate([query, mark_q], axis=1),
-                    jnp.concatenate([key, mark_k], axis=1),
-                )
-                peak = jnp.max(scores, axis=-1, keepdims=True)
-                weight = jnp.exp(scores - peak).astype(BF16)
-                total = dot(weight, value)
-                over = jnp.where(low, total[:group, :lanes], total[group:, :lanes])
-                under = jnp.where(low, total[:group, lanes:], total[group:, lanes:])
-                heads[index, rows, tile(at_tile)] = over / under
+            asked = slice(start + first, start + last)
+            mark_q = marks_q[index, asked, :]
+            query = qkv[index, asked, tile(at_tile)]
+            query = jnp.concatenate([query * head_masks[0], query * head_masks[1]], axis=0)
+            key = qkv[index, rows, tile(lane_tiles + at_tile)]
+            return dot_t(
+                jnp.concatenate([query, jnp.concatenate([mark_q, mark_q], axis=0)], axis=1),
+                jnp.concatenate([key, marks_k[index, rows, :]], axis=1),
+            )
+
+        def weigh(scores):
+            peak = jnp.max(scores, axis=-1, keepdims=True)
+            return jnp.exp(scores - peak).astype(BF16)
+
+        def mix(start, at_tile, weight):
+            rows = slice(start, start + group)
+            value = qkv[index, rows, tile(2 * lane_tiles + at_tile)]
+            total = dot(weight, jnp.concatenate([value, ones], axis=1))
+            over = jnp.where(low, total[:size, :lanes], total[size:, :lanes])
+            under = jnp.where(low, total[:size, lanes:], total[size:, lanes:])
+            asked = slice(start + first, start + last)
+            heads[index, asked, tile(at_tile)] = over / under
+
+        for at_job in range(len(jobs) + 2):
+            if at_job < len(jobs):
+                scored[at_job] = score(*jobs[at_job])
+            if 0 <= at_job - 1 < len(jobs):
+                weighted[at_job - 1] = weigh(scored.pop(at_job - 1))
+            if at_job >= 2:
+                mix(*jobs[at_job - 2], weighted.pop(at_job - 2))
 
     def gather(source, parts):
         pieces = []
@@ -289,7 +318,8 @@
                     backward[result[1] * HALF_ROW + row].start()
 
     def load_first(u):
-        inputs[u].wait()
+        if u:
+            inputs[u].wait()
         for spot in range(window_spots):
             row, col = divmod(spot, columns)
             place = (col // HALF_COLUMN) * 2 + row // HALF_ROW
@@ -319,32 +349,35 @@
                     group_at * QUARTER : (group_at + 1) * QUARTER
                 ]
 
+    inputs[0].wait()
     load_first(0)
     inputs[2].wait()
     inputs[3].wait()
     inputs[4].wait()
     mark(0, 0, own_regions(0))
     inputs[5].wait()
-    project(0, 0)
+    project(0, 0, whole, True)
     pl.semaphore_wait(barrier, 6)
     for copy in labels:
         copy.start()
-    for at in range(4, 8):
-        weights[at].start()
-    attend(0, 0)
+    attend(0, 0, 0, cut)
     inputs[6].wait()
     h = mlp(0, gather(xs, [(0, 0)]), gather(heads, [(0, 0)]).astype(BF16), True)
     finish_first(0, h, (0, 2))
     forward[0].start()
     forward[1].start()
+    for at in range(4, 8):
+        weights[at].start()
     load_first(1)
     mark(0, 1, own_regions(1))
-    project(0, 1)
-    attend(0, 1)
+    project(0, 1, whole)
+    attend(0, 1, 0, cut)
     h = mlp(0, gather(xs, [(1, 0)]), gather(heads, [(1, 0)]).astype(BF16))
     finish_first(1, h, (4, 6))
     forward[2].start()
     forward[3].start()
+    attend(0, 0, cut, group)
+    attend(0, 1, cut, group)
     parts = [(0, 1), (1, 1)]
     h = mlp(0, gather(xs, parts), gather(heads, parts).astype(BF16))
     finish_first(0, h[:group], (1, 3))
@@ -354,15 +387,16 @@
     for copy in labels:
         copy.wait_recv()
     load_second(0, (2, 3))
+    project(1, 0, near, True)
     mark(1, 0, [(side, 0), (side, HALF_ROW), (region, HALF_ROW), (region, 2 * HALF_ROW)])
     mark(1, 1, [(side, 2 * HALF_ROW), (corner, 0), (below, 0), (region, 3 * HALF_ROW)])
     load_second(0, (0, 1))
-    project(1, 0)
+    project(1, 0, far)
     attend(1, 0)
     o_send[...] = gather(heads, [(2, 0)]).astype(BF16)
     outward.start()
     load_second(1, (0, 1, 2, 3))
-    project(1, 1)
+    project(1, 1, whole)
     attend(1, 1)
     h = mlp(1, gather(xs, [(3, 0)]), gather(heads, [(3, 0)]).astype(BF16), True)
     finish_second(0, h, (("send", 0), ("send", 1)))

time: 29.4 us -> 28.9 us (0.983)
  Pallas kernels: 29.2 us -> 28.5 us
    pallas_call x1, Pallas kernels: 28.3 us -> 27.6 us  [per_device(): pl.pallas_call(kernel, out_shape=pltpu.VMEM(x.shape, BF16), in_specs=[hbm...]
where the time goes in v4:
time: 28.9 us; the launch traced here: 28.7 us
  Pallas kernels  28.5 us (99%)
    pallas_call x1, Pallas kernels, per_device(): pl.pallas_call(kernel, out_shape=pltpu.VMEM(x.shape, BF16), in_specs=[hbm...  27.6 us
    pallas_call x1, Pallas kernels, per_device(): pl.pallas_call(settle, out_shape=jax.ShapeDtypeStruct(x.shape, BF16), in_...  0.88 us

profile of v4, /device:TPU:0, one launch (start us, length us, event | category | flops | bytes accessed | tf_op | source)
XLA Modules:
  0.0 28.7 jit_solution(4627813496647694338)
XLA Ops:
  0.0 27.6 %shard_map.100.source = bf16[144,4,4,128]{3,2,1,0:T(4,128)(2,1)S(1)} custom-call(bf16[144,4,4,128]{3,2,1,0:T(4,128)(2,1)} %bitcast.7, s32[12,4,12]{2,1,0:T(4,128)} %bitcast.8, bf16[2,288,128]{2,1,0:T(8,128)(2,1)} %constant.4.clone.select_hbm, f32[288,128]{1,0:T(8,128)} %constant.5.clone.column_hbm, f32[2,512]{1,0:T(2,128)} %g1_hbm.1, f32[2,512]{1,0:T(2,128)} %g2_hbm.1, ...), custom_call_target="tpu_custom_call" | custom-call | tf_op jit(solution)/shard_map/pallas_call | solution.py:452
  27.6 0.9 %shard_map.101 = bf16[144,4,4,128]{3,2,1,0:T(4,128)(2,1)} custom-call(bf16[144,4,4,128]{3,2,1,0:T(4,128)(2,1)S(1)} %shard_map.100.source), custom_call_target="tpu_custom_call" | custom-call | tf_op jit(solution)/shard_map/pallas_call | solution.py:504

commit v5 on v4

--- a/solution.py
+++ b/solution.py
@@ -400,17 +400,18 @@
     attend(1, 1)
     h = mlp(1, gather(xs, [(3, 0)]), gather(heads, [(3, 0)]).astype(BF16), True)
     finish_second(0, h, (("send", 0), ("send", 1)))
-    parts = [(3, 1), (2, 1)]
-    h = mlp(1, gather(xs, parts), gather(heads, parts).astype(BF16))
-    finish_second(1, h[:group], (("send", 2), ("out", 7)))
-    finish_second(0, h[group:], (("out", 3), ("out", 5)))
+    h = mlp(1, gather(xs, [(3, 1)]), gather(heads, [(3, 1)]).astype(BF16))
+    finish_second(1, h, (("send", 2), ("out", 7)))
     pieces = [own[2].astype(F32), own[4].astype(F32)]
-    residual = jnp.concatenate(
-        [piece[:QUARTER] for piece in pieces] + [piece[QUARTER:] for piece in pieces], axis=0
+    residual = [piece[:QUARTER] for piece in pieces] + [piece[QUARTER:] for piece in pieces]
+    outward.wait_recv()
+    h = mlp(
+        1,
+        jnp.concatenate([gather(xs, [(2, 1)])] + residual, axis=0),
+        jnp.concatenate([gather(heads, [(2, 1)]).astype(BF16), o_back[...]], axis=0),
     )
-    outward.wait_recv()
-    h = mlp(1, residual, o_back[...])
-    finish_second(1, h, (("out", 2), ("out", 4)))
+    finish_second(0, h[:group], (("out", 3), ("out", 5)))
+    finish_second(1, h[group:], (("out", 2), ("out", 4)))
     for copy in backward:
         copy.wait_recv()
     for copy in labels + forward + [outward] + backward:

time: 28.9 us -> 28.8 us (level)
  no operation moved by 1% of the time
where the time goes in v5:
time: 28.8 us; the launch traced here: 28.5 us
  Pallas kernels  28.5 us (99%)
    pallas_call x1, Pallas kernels, per_device(): pl.pallas_call(kernel, out_shape=pltpu.VMEM(x.shape, BF16), in_specs=[hbm...  27.6 us
    pallas_call x1, Pallas kernels, per_device(): pl.pallas_call(settle, out_shape=jax.ShapeDtypeStruct(x.shape, BF16), in_...  0.88 us

profile of v5, /device:TPU:0, one launch (start us, length us, event | category | flops | bytes accessed | tf_op | source)
XLA Modules:
  0.0 28.5 jit_solution(13942377854667332341)
XLA Ops:
  0.0 27.6 %shard_map.100.source = bf16[144,4,4,128]{3,2,1,0:T(4,128)(2,1)S(1)} custom-call(bf16[144,4,4,128]{3,2,1,0:T(4,128)(2,1)} %bitcast.7, s32[12,4,12]{2,1,0:T(4,128)} %bitcast.8, bf16[2,288,128]{2,1,0:T(8,128)(2,1)} %constant.4.clone.select_hbm, f32[288,128]{1,0:T(8,128)} %constant.5.clone.column_hbm, f32[2,512]{1,0:T(2,128)} %g1_hbm.1, f32[2,512]{1,0:T(2,128)} %g2_hbm.1, ...), custom_call_target="tpu_custom_call" | custom-call | tf_op jit(solution)/shard_map/pallas_call | solution.py:453
  27.6 0.9 %shard_map.101 = bf16[144,4,4,128]{3,2,1,0:T(4,128)(2,1)} custom-call(bf16[144,4,4,128]{3,2,1,0:T(4,128)(2,1)S(1)} %shard_map.100.source), custom_call_target="tpu_custom_call" | custom-call | tf_op jit(solution)/shard_map/pallas_call | solution.py:505

commit v6 on v4

--- a/solution.py
+++ b/solution.py
@@ -88,7 +88,7 @@
     group = span // 2
     half = group // 2
     hidden = wup.shape[2]
-    step = 256
+    step = 512
     columns = 2 * HALF_COLUMN
     window_spots = spots // 2
 

time: 28.9 us -> 28.9 us (level)
  no operation moved by 1% of the time
where the time goes in v6:
time: 28.9 us; the launch traced here: 28.7 us
  Pallas kernels  28.5 us (99%)
    pallas_call x1, Pallas kernels, per_device(): pl.pallas_call(kernel, out_shape=pltpu.VMEM(x.shape, BF16), in_specs=[hbm...  27.6 us
    pallas_call x1, Pallas kernels, per_device(): pl.pallas_call(settle, out_shape=jax.ShapeDtypeStruct(x.shape, BF16), in_...  0.88 us

profile of v6, /device:TPU:0, one launch (start us, length us, event | category | flops | bytes accessed | tf_op | source)
XLA Modules:
  0.0 28.7 jit_solution(4627813496647694338)
XLA Ops:
  0.0 27.6 %shard_map.100.source = bf16[144,4,4,128]{3,2,1,0:T(4,128)(2,1)S(1)} custom-call(bf16[144,4,4,128]{3,2,1,0:T(4,128)(2,1)} %bitcast.7, s32[12,4,12]{2,1,0:T(4,128)} %bitcast.8, bf16[2,288,128]{2,1,0:T(8,128)(2,1)} %constant.4.clone.select_hbm, f32[288,128]{1,0:T(8,128)} %constant.5.clone.column_hbm, f32[2,512]{1,0:T(2,128)} %g1_hbm.1, f32[2,512]{1,0:T(2,128)} %g2_hbm.1, ...), custom_call_target="tpu_custom_call" | custom-call | tf_op jit(solution)/shard_map/pallas_call | solution.py:452
  27.6 0.9 %shard_map.101 = bf16[144,4,4,128]{3,2,1,0:T(4,128)(2,1)} custom-call(bf16[144,4,4,128]{3,2,1,0:T(4,128)(2,1)S(1)} %shard_map.100.source), custom_call_target="tpu_custom_call" | custom-call | tf_op jit(solution)/shard_map/pallas_call | solution.py:504
